TPU v7x, 32 devices: a whole 2x2x4 slice. The times are simulated.
32 devices in a mesh: grp: 2 (over y), blk: 16 (over z, x, core).
Axes of the slice: x: 2, y: 2, z: 4, core: 2. Of those that a mesh axis runs over, the one named last changes fastest.
Arguments:
- query_rows: bfloat16 [3072, 4096], P('blk', 'grp'), may hold values from -128 to 128
- key_rows: bfloat16 [3072, 512], P(('grp', 'blk')), may hold values from -6 to 6
- value_rows: bfloat16 [3072, 512], P(('grp', 'blk')), may hold values from -6 to 6
- span_ids: int32 [32], P('blk'), may hold values from 0 to 31, as said below
Outputs:
- attended: bfloat16 [3072, 4096], P('blk', 'grp')
Inputs may be any that keep to these rules, and one draw needn't show every extreme that they name: `span_ids`: A permutation of 0 to 31; each device of blk holds two entries, in device order.
All inputs are finite; a program needn't handle non-finite values.
Results may differ from a plain program's by a relative error of at most 0.0045.
Values may be sent and summed in bfloat16 or wider, within the bound.
A program may use at most 64 MiB of HBM per device.

v0:
```python
import jax
import jax.numpy as jnp
from jax import lax
from jax.sharding import PartitionSpec as P

HEAD_DIM = 128


def safe_top(values):
    return jnp.where(values == -jnp.inf, 0.0, values)


def attend(state, query_heads, query_pos, keys_block, values_block, key_pos):
    mark, total, weighted = state
    scale = query_heads.shape[-1] ** (-0.5)
    scores = (
        jnp.einsum("tgrd,ngd->grtn", query_heads, keys_block, preferred_element_type=jnp.float32)
        * scale
    )
    allowed = key_pos[None, :] <= query_pos[:, None]
    scores = jnp.where(allowed, scores, -jnp.inf)
    fresh = jnp.maximum(mark, jnp.max(scores, axis=-1))
    steady = safe_top(fresh)
    factor = jnp.exp(mark - steady)
    weights = jnp.where(allowed, jnp.exp(scores - steady[..., None]), 0.0).astype(jnp.bfloat16)
    total = total * factor + jnp.sum(weights.astype(jnp.float32), axis=-1)
    update = jnp.einsum("grtn,ngd->grtd", weights, values_block, preferred_element_type=jnp.float32)
    weighted = weighted * factor[..., None] + update
    return (fresh, total, weighted)


def lookup_ids(table, indices):
    columns = jnp.arange(table.shape[0], dtype=jnp.int32)
    matches = indices[:, None] == columns[None, :]
    return jnp.sum(jnp.where(matches, table[None, :], 0), axis=1)


def pick_width(count, limit):
    chosen = 1
    for trial in range(1, min(count, limit) + 1):
        if count % trial == 0:
            chosen = trial
    return chosen


def fold_keys(state_in, piece, query_heads, query_pos, table, locate, span_len, limit):
    count = piece.shape[1]
    width = pick_width(count, limit)
    steps_count = count // width
    pieces = jnp.moveaxis(piece.reshape((2, steps_count, width) + piece.shape[2:]), 1, 0)
    offsets = jnp.arange(steps_count, dtype=jnp.int32) * width

    def step(carry, item):
        pair_now, offset = item
        gathered = offset + jnp.arange(width, dtype=jnp.int32)
        stored = locate(gathered)
        key_pos = lookup_ids(table, stored // span_len) * span_len + stored % span_len
        result = attend(carry, query_heads, query_pos, pair_now[0], pair_now[1], key_pos)
        return (result, None)

    return lax.scan(step, state_in, (pieces, offsets))[0]


def empty_state(kv_count, per_kv, tokens):
    return (
        jnp.full((kv_count, per_kv, tokens), -jnp.inf, jnp.float32),
        jnp.zeros((kv_count, per_kv, tokens), jnp.float32),
        jnp.zeros((kv_count, per_kv, tokens, HEAD_DIM), jnp.float32),
    )


def body(query_rows, key_rows, value_rows, span_ids):
    tokens = query_rows.shape[0]
    span_len = tokens // 2
    kv_heads = key_rows.shape[1] // HEAD_DIM
    key_count = key_rows.shape[0]
    groups = lax.axis_size("grp")
    blocks = lax.axis_size("blk")
    blk_here = lax.axis_index("blk")
    table = lax.all_gather(span_ids, "blk", axis=0, tiled=True)
    own_ids = lax.dynamic_slice_in_dim(table, blk_here * 2, 2, 0)
    query_pos = (
        own_ids[:, None] * span_len + jnp.arange(span_len, dtype=jnp.int32)[None, :]
    ).reshape(-1)
    own_heads = query_rows.shape[1] // HEAD_DIM
    heads = own_heads * groups
    ratio = heads // kv_heads
    kv_own = max(1, own_heads // ratio)
    per_kv = own_heads // kv_own
    key_parts = []
    value_parts = []
    for target in range(groups):
        first = target * own_heads // ratio
        key_parts.append(key_rows[:, first * HEAD_DIM : (first + kv_own) * HEAD_DIM])
        value_parts.append(value_rows[:, first * HEAD_DIM : (first + kv_own) * HEAD_DIM])
    routed_keys, routed_values = (
        lax.all_to_all(jnp.stack(key_parts), "grp", split_axis=0, concat_axis=1, tiled=True),
        lax.all_to_all(jnp.stack(value_parts), "grp", split_axis=0, concat_axis=1, tiled=True),
    )
    paired = jnp.stack([routed_keys[0], routed_values[0]]).reshape(
        2, groups * key_count, kv_own, HEAD_DIM
    )
    query_heads = query_rows.reshape(tokens, kv_own, per_kv, HEAD_DIM)
    group_rows = groups * key_count

    def locate(gathered):
        source_blk = gathered // group_rows
        within = gathered % group_rows
        source_grp = within // key_count
        slot_row = within % key_count
        return ((source_grp * blocks + source_blk) * key_count + slot_row).astype(jnp.int32)

    state = fold_keys(
        empty_state(kv_own, per_kv, tokens),
        lax.all_gather(paired, "blk", axis=1, tiled=True),
        query_heads,
        query_pos,
        table,
        locate,
        span_len,
        512,
    )
    mark, total, weighted = state
    mixed = weighted / total[..., None]
    mixed = jnp.transpose(mixed, (2, 0, 1, 3)).reshape(tokens, own_heads * HEAD_DIM)
    return mixed.astype(jnp.bfloat16)


def solution(mesh):
    in_specs = (P("blk", "grp"), P(("grp", "blk"), None), P(("grp", "blk"), None), P("blk"))
    out_specs = P("blk", "grp")
    return jax.shard_map(body, mesh=mesh, in_specs=in_specs, out_specs=out_specs, check_vma=False)
```

profile of v0, /device:TPU:0, one launch (start us, length us, event | category | flops | bytes accessed | tf_op | source)
XLA Modules:
  0.0 138.3 jit_solution(15615476927728508277)
XLA Ops:
  8.0 4.3 %all-to-all-start = ((bf16[2,96,256]{2,1,0:T(8,128)(2,1)}), bf16[2,96,256]{2,1,0:T(8,128)(2,1)S(1)}, u32[]{:S(2)}, u32[]{:S(2)}) async-start(bf16[2,96,256]{2,1,0:T(8,128)(2,1)} %pad_maximum_fusion.1), calls=%async_computation | async-start | bytes 196608 | tf_op jit(solution)/shard_map/all_to_all | solution.py:97
  13.7 2.9 %all-to-all-done = bf16[2,96,256]{2,1,0:T(8,128)(2,1)S(1)} async-done(((bf16[2,96,256]{2,1,0:T(8,128)(2,1)}), bf16[2,96,256]{2,1,0:T(8,128)(2,1)S(1)}, u32[]{:S(2)}, u32[]{:S(2)}) %all-to-all-start) | async-done | bytes 98336 | tf_op jit(solution)/shard_map/all_to_all | solution.py:97
  16.6 3.3 %all-to-all-start.1 = ((bf16[2,96,256]{2,1,0:T(8,128)(2,1)}), bf16[2,96,256]{2,1,0:T(8,128)(2,1)S(1)}, u32[]{:S(2)}, u32[]{:S(2)}) async-start(bf16[2,96,256]{2,1,0:T(8,128)(2,1)} %pad_maximum_fusion.2), calls=%async_computation.1 | async-start | bytes 196608 | tf_op jit(solution)/shard_map/all_to_all | solution.py:98
  20.0 4.2 %all-to-all-done.1 = bf16[2,96,256]{2,1,0:T(8,128)(2,1)S(1)} async-done(((bf16[2,96,256]{2,1,0:T(8,128)(2,1)}), bf16[2,96,256]{2,1,0:T(8,128)(2,1)S(1)}, u32[]{:S(2)}, u32[]{:S(2)}) %all-to-all-start.1) | async-done | bytes 98336 | tf_op jit(solution)/shard_map/all_to_all | solution.py:98
  25.3 1.3 copy.20
  26.8 1.3 dynamic-slice
  29.6 12.8 %all-reduce = s32[32]{0:T(128)S(1)} all-reduce(s32[32]{0:T(128)S(1)} %dynamic-update-slice), channel_id=1, replica_groups=mesh['grp'=2,'blk'=16] {'blk'}, use_global_device_ids=true, to_apply=%add | all-reduce | flops 32 | bytes 256
  42.5 29.2 %all-gather.2.cloned.1.call-done = bf16[2,3072,2,128]{3,2,1,0:T(2,128)(2,1)} async-done(((bf16[2,192,2,128]{3,2,1,0:T(2,128)(2,1)}), bf16[2,3072,2,128]{3,2,1,0:T(2,128)(2,1)}) %all-gather.2.cloned.1.call-update) | async-done | bytes 3145744 | tf_op jit(solution)/shard_map/all_gather | solution.py:115
  71.7 4.0 %copy.13 = bf16[2,3072,2,128]{3,1,2,0:T(8,128)(2,1)} copy(bf16[2,3072,2,128]{3,2,1,0:T(2,128)(2,1)} %all-gather.2.cloned.1.call-done) | data formatting | bytes 6291456 | tf_op jit(solution)/shard_map/all_gather | solution.py:115
  75.7 53.7 %while.18 = (s32[]{:T(128)}, f32[2,8,192]{2,1,0:T(8,128)S(1)}, f32[2,8,192]{2,1,0:T(8,128)S(1)}, f32[2,8,192,128]{3,2,1,0:T(8,128)S(1)}, s32[6]{0:T(128)S(1)}, /...) while((s32[]{:T(128)}, f32[2,8,192]{2,1,0:T(8,128)S(1)}, ...), condition=%wide.region_4.5_spmd.clone, body=%wide.region_0.4_spmd.clone.sunk | while | flops 830291648 | bytes 25005344 | solution.py:61
  78.0 1.1 dynamic-slice_bitcast_fusion.2
  79.1 1.1 fusion.25
  80.2 2.0 %convert_reduce_fusion.2 = f32[2,8,192]{2,1,0:T(8,128)S(1)} fusion(f32[2,8,192]{2,1,0:T(8,128)S(1)} %get-tuple-element.315, f32[2,512,192,8]{1,2,3,0:T(8,128)S(1)} %get-tuple-element.316, pred[192,512]{1,0:T(8,128)(4,1)S(1)} %broadcast_compare_fusion.2), kind=kLoop, calls=%fused_computation.2.clone.1 | loop fusion | flops 11006976 | bytes 6414336 | tf_op jit(solution)/shard_map/while/body/eval_jaxpr/reduce_sum | solution.py:26
  82.3 2.3 %fusion.27 = f32[2,8,192,128]{3,2,1,0:T(8,128)S(1)} fusion(f32[2,8,192,128]{3,2,1,0:T(8,128)S(1)} %get-tuple-element.333, f32[2,8,192]{2,1,0:T(8,128)S(1)} %get-tuple-element.318, pred[]{:T(512)S(6)} %compare.3, bf16[1,2,512,2,128]{4,2,3,1,0:T(8,128)(2,1)S(1)} %dynamic-slice_bitcast_fusion.2, f32[2,512,192,8]{1,2,3,0:T(8,128)S(1)} %get-tuple-element.316, ...), kind=kOutput, calls=%fused_computation.6.clone.1 | convolution fusion | flops 411697152 | bytes 9830401 | tf_op jit(solution)/shard_map/while/body/eval_jaxpr/grtn,ngd->grtd/dot_general | solution.py:27
  88.0 1.1 fusion.25
  89.2 2.0 %convert_reduce_fusion.2 = f32[2,8,192]{2,1,0:T(8,128)S(1)} fusion(f32[2,8,192]{2,1,0:T(8,128)S(1)} %get-tuple-element.315, f32[2,512,192,8]{1,2,3,0:T(8,128)S(1)} %get-tuple-element.316, pred[192,512]{1,0:T(8,128)(4,1)S(1)} %broadcast_compare_fusion.2), kind=kLoop, calls=%fused_computation.2.clone.1 | loop fusion | flops 11006976 | bytes 6414336 | tf_op jit(solution)/shard_map/while/body/eval_jaxpr/reduce_sum | solution.py:26
  91.2 2.3 %fusion.27 = f32[2,8,192,128]{3,2,1,0:T(8,128)S(1)} fusion(f32[2,8,192,128]{3,2,1,0:T(8,128)S(1)} %get-tuple-element.333, f32[2,8,192]{2,1,0:T(8,128)S(1)} %get-tuple-element.318, pred[]{:T(512)S(6)} %compare.3, bf16[1,2,512,2,128]{4,2,3,1,0:T(8,128)(2,1)S(1)} %dynamic-slice_bitcast_fusion.2, f32[2,512,192,8]{1,2,3,0:T(8,128)S(1)} %get-tuple-element.316, ...), kind=kOutput, calls=%fused_computation.6.clone.1 | convolution fusion | flops 411697152 | bytes 9830401 | tf_op jit(solution)/shard_map/while/body/eval_jaxpr/grtn,ngd->grtd/dot_general | solution.py:27
  95.9 1.1 dynamic-slice_bitcast_fusion.2
  97.0 1.1 fusion.25
  98.1 2.0 %convert_reduce_fusion.2 = f32[2,8,192]{2,1,0:T(8,128)S(1)} fusion(f32[2,8,192]{2,1,0:T(8,128)S(1)} %get-tuple-element.315, f32[2,512,192,8]{1,2,3,0:T(8,128)S(1)} %get-tuple-element.316, pred[192,512]{1,0:T(8,128)(4,1)S(1)} %broadcast_compare_fusion.2), kind=kLoop, calls=%fused_computation.2.clone.1 | loop fusion | flops 11006976 | bytes 6414336 | tf_op jit(solution)/shard_map/while/body/eval_jaxpr/reduce_sum | solution.py:26
  100.2 2.3 %fusion.27 = f32[2,8,192,128]{3,2,1,0:T(8,128)S(1)} fusion(f32[2,8,192,128]{3,2,1,0:T(8,128)S(1)} %get-tuple-element.333, f32[2,8,192]{2,1,0:T(8,128)S(1)} %get-tuple-element.318, pred[]{:T(512)S(6)} %compare.3, bf16[1,2,512,2,128]{4,2,3,1,0:T(8,128)(2,1)S(1)} %dynamic-slice_bitcast_fusion.2, f32[2,512,192,8]{1,2,3,0:T(8,128)S(1)} %get-tuple-element.316, ...), kind=kOutput, calls=%fused_computation.6.clone.1 | convolution fusion | flops 411697152 | bytes 9830401 | tf_op jit(solution)/shard_map/while/body/eval_jaxpr/grtn,ngd->grtd/dot_general | solution.py:27
  106.0 1.1 fusion.25
  107.1 2.0 %convert_reduce_fusion.2 = f32[2,8,192]{2,1,0:T(8,128)S(1)} fusion(f32[2,8,192]{2,1,0:T(8,128)S(1)} %get-tuple-element.315, f32[2,512,192,8]{1,2,3,0:T(8,128)S(1)} %get-tuple-element.316, pred[192,512]{1,0:T(8,128)(4,1)S(1)} %broadcast_compare_fusion.2), kind=kLoop, calls=%fused_computation.2.clone.1 | loop fusion | flops 11006976 | bytes 6414336 | tf_op jit(solution)/shard_map/while/body/eval_jaxpr/reduce_sum | solution.py:26
  109.2 2.3 %fusion.27 = f32[2,8,192,128]{3,2,1,0:T(8,128)S(1)} fusion(f32[2,8,192,128]{3,2,1,0:T(8,128)S(1)} %get-tuple-element.333, f32[2,8,192]{2,1,0:T(8,128)S(1)} %get-tuple-element.318, pred[]{:T(512)S(6)} %compare.3, bf16[1,2,512,2,128]{4,2,3,1,0:T(8,128)(2,1)S(1)} %dynamic-slice_bitcast_fusion.2, f32[2,512,192,8]{1,2,3,0:T(8,128)S(1)} %get-tuple-element.316, ...), kind=kOutput, calls=%fused_computation.6.clone.1 | convolution fusion | flops 411697152 | bytes 9830401 | tf_op jit(solution)/shard_map/while/body/eval_jaxpr/grtn,ngd->grtd/dot_general | solution.py:27
  113.8 1.1 dynamic-slice_bitcast_fusion.2
  114.9 1.1 fusion.25
  116.1 2.0 %convert_reduce_fusion.2 = f32[2,8,192]{2,1,0:T(8,128)S(1)} fusion(f32[2,8,192]{2,1,0:T(8,128)S(1)} %get-tuple-element.315, f32[2,512,192,8]{1,2,3,0:T(8,128)S(1)} %get-tuple-element.316, pred[192,512]{1,0:T(8,128)(4,1)S(1)} %broadcast_compare_fusion.2), kind=kLoop, calls=%fused_computation.2.clone.1 | loop fusion | flops 11006976 | bytes 6414336 | tf_op jit(solution)/shard_map/while/body/eval_jaxpr/reduce_sum | solution.py:26
  118.1 2.3 %fusion.27 = f32[2,8,192,128]{3,2,1,0:T(8,128)S(1)} fusion(f32[2,8,192,128]{3,2,1,0:T(8,128)S(1)} %get-tuple-element.333, f32[2,8,192]{2,1,0:T(8,128)S(1)} %get-tuple-element.318, pred[]{:T(512)S(6)} %compare.3, bf16[1,2,512,2,128]{4,2,3,1,0:T(8,128)(2,1)S(1)} %dynamic-slice_bitcast_fusion.2, f32[2,512,192,8]{1,2,3,0:T(8,128)S(1)} %get-tuple-element.316, ...), kind=kOutput, calls=%fused_computation.6.clone.1 | convolution fusion | flops 411697152 | bytes 9830401 | tf_op jit(solution)/shard_map/while/body/eval_jaxpr/grtn,ngd->grtd/dot_general | solution.py:27
  122.8 1.1 dynamic-slice_bitcast_fusion.2
  123.9 1.1 fusion.25
  125.0 2.0 %convert_reduce_fusion.2 = f32[2,8,192]{2,1,0:T(8,128)S(1)} fusion(f32[2,8,192]{2,1,0:T(8,128)S(1)} %get-tuple-element.315, f32[2,512,192,8]{1,2,3,0:T(8,128)S(1)} %get-tuple-element.316, pred[192,512]{1,0:T(8,128)(4,1)S(1)} %broadcast_compare_fusion.2), kind=kLoop, calls=%fused_computation.2.clone.1 | loop fusion | flops 11006976 | bytes 6414336 | tf_op jit(solution)/shard_map/while/body/eval_jaxpr/reduce_sum | solution.py:26
  127.1 2.3 %fusion.27 = f32[2,8,192,128]{3,2,1,0:T(8,128)S(1)} fusion(f32[2,8,192,128]{3,2,1,0:T(8,128)S(1)} %get-tuple-element.333, f32[2,8,192]{2,1,0:T(8,128)S(1)} %get-tuple-element.318, pred[]{:T(512)S(6)} %compare.3, bf16[1,2,512,2,128]{4,2,3,1,0:T(8,128)(2,1)S(1)} %dynamic-slice_bitcast_fusion.2, f32[2,512,192,8]{1,2,3,0:T(8,128)S(1)} %get-tuple-element.316, ...), kind=kOutput, calls=%fused_computation.6.clone.1 | convolution fusion | flops 411697152 | bytes 9830401 | tf_op jit(solution)/shard_map/while/body/eval_jaxpr/grtn,ngd->grtd/dot_general | solution.py:27
  (82 shorter events, 23.5 us)
Async XLA Ops:
  8.0 8.6 %all-to-all-start = ((bf16[2,96,256]{2,1,0:T(8,128)(2,1)}), bf16[2,96,256]{2,1,0:T(8,128)(2,1)S(1)}, u32[]{:S(2)}, u32[]{:S(2)}) async-start(bf16[2,96,256]{2,1,0:T(8,128)(2,1)} %pad_maximum_fusion.1), calls=%async_computation | async-start | bytes 196608 | tf_op jit(solution)/shard_map/all_to_all | solution.py:97
  16.6 7.6 %all-to-all-start.1 = ((bf16[2,96,256]{2,1,0:T(8,128)(2,1)}), bf16[2,96,256]{2,1,0:T(8,128)(2,1)S(1)}, u32[]{:S(2)}, u32[]{:S(2)}) async-start(bf16[2,96,256]{2,1,0:T(8,128)(2,1)} %pad_maximum_fusion.2), calls=%async_computation.1 | async-start | bytes 196608 | tf_op jit(solution)/shard_map/all_to_all | solution.py:98
  19.9 51.8 %all-gather.2.cloned.1.call-start = ((), (), s32[]{:S(2)}) async-start(), calls=%async_computation.2 | async-start | bytes 3342336 | tf_op jit(solution)/shard_map/all_gather | solution.py:115
Sparse Core Ops, SparseCore 0:
  25.4 46.3 all-gather.1
where the time goes:
time: 139 us; the launch traced here: 138 us
  waiting for transfers between devices  36.3 us (26%)
  other arithmetic  24.9 us (18%)
  local copies, waits for them, and re-layouts  21.5 us (15%)
  matrix products  20.7 us (15%)
  between operations  14.1 us (10%)
  blocking collectives  12.8 us (9%)
  starting transfers between devices  7.64 us (5%)
    all_gather x1, waiting for transfers between devices, body(): lax.all_gather(paired, 'blk', axis=1, tiled=True)  29.2 us
    dot_general x6, matrix products, attend(): jnp.einsum('grtn,ngd->grtd', weights, values_block, preferred_element_typ...  13.9 us
    unnamed x1, blocking collectives  12.8 us
    reduce_sum x6, other arithmetic, attend(): total = total * factor + jnp.sum(weights.astype(jnp.float32), axis=-1)  12 us
    dynamic_slice x12, local copies, waits for them, and re-layouts, fold_keys(): return lax.scan(step, state_in, (pieces, offsets))[0]  10 us
    dot_general x6, matrix products, attend(): jnp.einsum('tgrd,ngd->grtn', query_heads, keys_block, preferred_element_t...  6.78 us
    unnamed x6, local copies, waits for them, and re-layouts  4.71 us
    all_to_all x1, starting transfers between devices, body(): lax.all_to_all(jnp.stack(key_parts), 'grp', split_axis=0, concat_axis=1,...  4.26 us
  transfers between devices with their start and end apart: 3, of which 3 were waited for; matrix products, arithmetic and copies ran while one was open for 4% of the time, Pallas kernels for 0%

commit v1 on v0

--- a/solution.py
+++ b/solution.py
@@ -1,7 +1,15 @@
+import functools
+import math
+
 import jax
 import jax.numpy as jnp
 from jax import lax
+from jax.experimental import pallas as pl
+from jax.experimental.pallas import tpu as pltpu
 from jax.sharding import PartitionSpec as P
+
+MESH = pl.DeviceIdType.MESH
+FAR = -1e30
 
 HEAD_DIM = 128
 
@@ -69,8 +77,345 @@
     )
 
 
+def fits_kernel(query_rows, key_rows):
+    groups, blocks = lax.axis_size("grp"), lax.axis_size("blk")
+    span_len = query_rows.shape[0] // 2
+    return (
+        groups == 2
+        and blocks % 4 == 0
+        and key_rows.shape[1] == 2 * groups * HEAD_DIM
+        and key_rows.shape[0] == span_len
+        and span_len % 16 == 0
+        and span_len < HEAD_DIM
+        and query_rows.shape[1] % (2 * HEAD_DIM) == 0
+    )
+
+
+def attention_kernel(
+    planes, span, per_kv, rows_at_once,
+    q_hbm, k_hbm, v_hbm, id_ref, out_ref,
+    kv, stage, ids, qraw, qaug_q, kp, vp, onehot, acc, mark, obuf,
+    load_sem, swap_send, swap_recv, id_send, id_recv, q_sem,
+    up_send, down_send, x_send, z_recv, x_recv, out_sem,
+):
+    y = lax.axis_index("grp")
+    blk = lax.axis_index("blk")
+    z, x, c = blk // 4, (blk // 2) % 2, blk % 2
+    blocks = 4 * planes
+    wide = per_kv * HEAD_DIM
+    rows = per_kv * span
+    keys = 8 * span
+    other_y, other_x, other_c = 1 - y, 1 - x, 1 - c
+    sibling = (y, z * 4 + x * 2 + other_c)
+    across = (y, z * 4 + other_x * 2 + c)
+
+    def place(at_z):
+        return (y, at_z * 4 + x * 2 + c)
+
+    def remote(src, dst, send, recv, target):
+        return pltpu.make_async_remote_copy(
+            src_ref=src, dst_ref=dst, send_sem=send, recv_sem=recv,
+            device_id=target, device_id_type=MESH,
+        )
+
+    def load(head, half):
+        source = (k_hbm, v_hbm)[half]
+        return pltpu.make_async_copy(
+            source.at[:, pl.ds(head * HEAD_DIM, HEAD_DIM)],
+            stage.at[head, :, pl.ds(half * HEAD_DIM, HEAD_DIM)],
+            load_sem.at[head, half],
+        )
+
+    def load_own(half):
+        source = (k_hbm, v_hbm)[half]
+        return pltpu.make_async_copy(
+            source.at[:, pl.ds(pl.multiple_of((2 * y + c) * HEAD_DIM, HEAD_DIM), HEAD_DIM)],
+            kv.at[z, x, y, c, :, pl.ds(half * HEAD_DIM, HEAD_DIM)],
+            load_sem.at[4, half],
+        )
+
+    for head in range(4):
+        for half in range(2):
+            load(head, half).start()
+    for half in range(2):
+        load_own(half).start()
+
+    barrier = pltpu.get_barrier_semaphore()
+
+    @pl.loop(1, blocks)
+    def _(step):
+        pl.semaphore_signal(
+            barrier, inc=1, device_id=(y, lax.rem(blk + step, blocks)), device_id_type=MESH
+        )
+
+    for target_c in (c, other_c):
+        pl.semaphore_signal(
+            barrier, inc=1, device_id=(other_y, z * 4 + x * 2 + target_c), device_id_type=MESH
+        )
+
+    token = lax.broadcasted_iota(jnp.int32, (span, HEAD_DIM), 0)
+    lane = lax.broadcasted_iota(jnp.int32, (span, HEAD_DIM), 1)
+    onehot[...] = jnp.where((lane == token) | (lane == span), 1.0, 0.0).astype(jnp.bfloat16)
+    penalty = jnp.where(
+        ((lane > token) & (lane < span)) | (lane == span), FAR, 0.0
+    ).astype(jnp.bfloat16)
+    for slot in range(4):
+        for r in range(per_kv):
+            qaug_q[slot, r * span : (r + 1) * span, HEAD_DIM:] = penalty
+    vp[:, HEAD_DIM:] = jnp.ones((keys, HEAD_DIM), jnp.bfloat16)
+    mark[...] = jnp.full(mark.shape, -3e38, jnp.float32)
+    acc[...] = jnp.zeros(acc.shape, jnp.float32)
+    for head in range(4):
+        for half in range(2):
+            load(head, half).wait()
+    for half in range(2):
+        load_own(half).wait()
+    pl.semaphore_wait(barrier, blocks + 1)
+
+    def swap(slot):
+        to_y = (y, other_y, other_y)[slot]
+        to_c = (other_c, c, other_c)[slot]
+        return remote(
+            stage.at[2 * to_y + to_c], kv.at[z, x, y, c],
+            swap_send.at[slot], swap_recv.at[slot], (to_y, z * 4 + x * 2 + to_c),
+        )
+
+    for slot in range(3):
+        swap(slot).start()
+
+    def id_copy(step):
+        return remote(
+            id_ref, ids.at[blk], id_send.at[step], id_recv.at[step],
+            (y, lax.rem(blk + step, blocks)),
+        )
+
+    own_id = pltpu.make_async_copy(id_ref, ids.at[blk], id_send.at[0])
+    own_id.start()
+
+    @pl.loop(1, blocks)
+    def _(step):
+        id_copy(step).start()
+
+    def q_columns(core):
+        return pl.ds(pl.multiple_of(core * wide, HEAD_DIM), wide)
+
+    q_away = remote(q_hbm.at[:, q_columns(other_c)], qraw.at[0], q_sem.at[0], q_sem.at[1], sibling)
+    q_here = pltpu.make_async_copy(q_hbm.at[:, q_columns(c)], qraw.at[1], q_sem.at[2])
+    q_away.start()
+    q_here.start()
+
+    def up(at_z, u):
+        chunk = kv.at[at_z, x, u]
+        return remote(chunk, chunk, up_send.at[at_z, u], z_recv.at[at_z, u], place(z + 1))
+
+    def down(at_z, u):
+        chunk = kv.at[at_z, x, u]
+        return remote(chunk, chunk, down_send.at[at_z, u], z_recv.at[at_z, u], place(z - 1))
+
+    def over(at_z, u):
+        chunk = kv.at[at_z, x, u]
+        return remote(chunk, chunk, x_send.at[at_z, u], x_recv.at[at_z, u], across)
+
+    def z_arrival(at_z, u):
+        chunk = kv.at[at_z, x, u]
+        return remote(chunk, chunk, up_send.at[at_z, u], z_recv.at[at_z, u], across)
+
+    def x_arrival(at_z, u):
+        chunk = kv.at[at_z, other_x, u]
+        return remote(chunk, chunk, x_send.at[at_z, u], x_recv.at[at_z, u], across)
+
+    def pass_on(at_z, u, from_below, from_above):
+        @pl.when(from_below & (z + 1 < planes))
+        def _():
+            up(at_z, u).start()
+
+        @pl.when(from_above & (z > 0))
+        def _():
+            down(at_z, u).start()
+
+        over(at_z, u).start()
+
+    swap(0).wait_recv()
+    pass_on(z, y, True, True)
+    swap(1).wait_recv()
+    swap(2).wait_recv()
+    pass_on(z, other_y, True, True)
+
+    def service(far, u):
+        @pl.when((far < planes) & (z - far >= 0))
+        def _():
+            z_arrival(z - far, u).wait_recv()
+            pass_on(z - far, u, True, False)
+
+        @pl.when((far < planes) & (z + far < planes))
+        def _():
+            z_arrival(z + far, u).wait_recv()
+            pass_on(z + far, u, False, True)
+
+    q_away.wait_recv()
+    q_here.wait()
+    for slot in range(4):
+        s = slot % 2
+        for r in range(per_kv):
+            qaug_q[slot, r * span : (r + 1) * span, :HEAD_DIM] = qraw[
+                slot // 2, s * span : (s + 1) * span, r * HEAD_DIM : (r + 1) * HEAD_DIM
+            ]
+    own_id.wait()
+
+    @pl.loop(1, blocks)
+    def _(step):
+        id_copy(step).wait_recv()
+
+    factor = HEAD_DIM ** (-0.5) * math.log2(math.e)
+    lane_row = lax.broadcasted_iota(jnp.int32, (1, HEAD_DIM), 1)
+    near = jnp.minimum(z, planes - 1 - z)
+    sign = jnp.where(z < planes - 1 - z, 1, -1)
+
+    def plane_of(k):
+        half = (k + 1) // 2
+        inner = z + jnp.where(k % 2 == 1, -half, half)
+        return jnp.where(k <= 2 * near, inner, z + sign * (k - near))
+
+    def finish(slot):
+        s = slot % 2
+        for r in range(per_kv):
+            both = acc[slot, r * span : (r + 1) * span, :]
+            obuf[slot // 2, pl.ds(pl.multiple_of(s * span, 16), span), r * HEAD_DIM : (r + 1) * HEAD_DIM] = (
+                both[:, :HEAD_DIM] / both[:, HEAD_DIM:]
+            ).astype(jnp.bfloat16)
+
+    out_away = remote(obuf.at[0], out_ref.at[:, q_columns(c)], out_sem.at[0], out_sem.at[1], sibling)
+    out_here = pltpu.make_async_copy(obuf.at[1], out_ref.at[:, q_columns(c)], out_sem.at[2])
+
+    @pl.loop(0, 4 * planes)
+    def _(t):
+        k, slot = t // 4, t % 4
+        p = plane_of(k)
+
+        @pl.when(slot == 0)
+        def _():
+            service(k + 1, y)
+            x_arrival(p, y).wait_recv()
+            x_arrival(p, other_y).wait_recv()
+            plane = kv[p].reshape(keys, 2 * HEAD_DIM)
+            kp[:, :HEAD_DIM] = plane[:, :HEAD_DIM]
+            vp[:, :HEAD_DIM] = plane[:, HEAD_DIM:]
+
+        @pl.when(slot == 2)
+        def _():
+            service(k + 1, other_y)
+
+        owner = z * 4 + x * 2 + jnp.where(slot < 2, other_c, c)
+        id_q = ids[owner, pl.ds(slot % 2, 1), :]
+        for j in range(8):
+            kx, ky, kc = j // 4, (j // 2) % 2, j % 2
+            id_k = ids[ky * (blocks // 2) + p * 2 + kx, kc : kc + 1, :]
+            same = jnp.where(id_k == id_q, 1.0, 0.0)
+            later = jnp.where(id_k > id_q, 1.0, 0.0)
+            choice = jnp.where(lane_row < span, same, later).astype(jnp.bfloat16)
+            kp[j * span : (j + 1) * span, HEAD_DIM:] = onehot[...] * choice
+
+        kmat = kp[...]
+        vmat = vp[...]
+        for first in range(0, rows, rows_at_once):
+            part = pl.ds(first, rows_at_once)
+            scores = lax.dot_general(
+                qaug_q[slot, part, :], kmat, (((1,), (1,)), ((), ())),
+                preferred_element_type=jnp.float32,
+            )
+            before = mark[slot, part, :]
+            fresh = jnp.maximum(before, jnp.max(scores, axis=1, keepdims=True))
+            mark[slot, part, :] = fresh
+            weights = jnp.exp2((scores - fresh[:, :1]) * factor).astype(jnp.bfloat16)
+            fade = jnp.exp2((before - fresh) * factor)
+            update = jnp.dot(weights, vmat, preferred_element_type=jnp.float32)
+            acc[slot, part, :HEAD_DIM] = acc[slot, part, :HEAD_DIM] * fade + update[:, :HEAD_DIM]
+            acc[slot, part, HEAD_DIM:] = acc[slot, part, HEAD_DIM:] * fade + update[:, HEAD_DIM:]
+
+        @pl.when(k == planes - 1)
+        def _():
+            finish(slot)
+
+        @pl.when((k == planes - 1) & (slot == 2))
+        def _():
+            out_away.start()
+
+    out_here.start()
+    for slot in range(3):
+        swap(slot).wait_send()
+    q_away.wait_send()
+
+    @pl.loop(1, blocks)
+    def _(step):
+        id_copy(step).wait_send()
+
+    @pl.loop(0, planes)
+    def _(at_z):
+        for u in range(2):
+            over(at_z, u).wait_send()
+
+            @pl.when((at_z <= z) & (z + 1 < planes))
+            def _():
+                up(at_z, u).wait_send()
+
+            @pl.when((at_z >= z) & (z > 0))
+            def _():
+                down(at_z, u).wait_send()
+
+    out_away.wait()
+    out_here.wait()
+
+
+def fused(query_rows, key_rows, value_rows, span_ids):
+    planes = lax.axis_size("blk") // 4
+    tokens, columns = query_rows.shape
+    span = tokens // 2
+    per_kv = columns // (2 * HEAD_DIM)
+    rows, keys, wide = per_kv * span, 8 * span, per_kv * HEAD_DIM
+    id_block = jnp.broadcast_to(jnp.tile(span_ids, 4)[:, None], (8, HEAD_DIM))
+    dma = pltpu.SemaphoreType.DMA
+    anywhere = pl.BlockSpec(memory_space=pl.ANY)
+    bf16, f32 = jnp.bfloat16, jnp.float32
+    return pl.pallas_call(
+        functools.partial(attention_kernel, planes, span, per_kv, math.gcd(rows, 256)),
+        out_shape=jax.ShapeDtypeStruct((tokens, columns), bf16),
+        in_specs=[anywhere] * 3 + [pl.BlockSpec(memory_space=pltpu.VMEM)],
+        out_specs=anywhere,
+        scratch_shapes=[
+            pltpu.VMEM((planes, 2, 2, 2, span, 2 * HEAD_DIM), bf16),
+            pltpu.VMEM((4, span, 2 * HEAD_DIM), bf16),
+            pltpu.VMEM((4 * planes, 8, HEAD_DIM), jnp.int32),
+            pltpu.VMEM((2, tokens, wide), bf16),
+            pltpu.VMEM((4, rows, 2 * HEAD_DIM), bf16),
+            pltpu.VMEM((keys, 2 * HEAD_DIM), bf16),
+            pltpu.VMEM((keys, 2 * HEAD_DIM), bf16),
+            pltpu.VMEM((span, HEAD_DIM), bf16),
+            pltpu.VMEM((4, rows, 2 * HEAD_DIM), f32),
+            pltpu.VMEM((4, rows, HEAD_DIM), f32),
+            pltpu.VMEM((2, tokens, wide), bf16),
+            dma((5, 2)),
+            dma((3,)),
+            dma((3,)),
+            dma((4 * planes,)),
+            dma((4 * planes,)),
+            dma((3,)),
+            dma((planes, 2)),
+            dma((planes, 2)),
+            dma((planes, 2)),
+            dma((planes, 2)),
+            dma((planes, 2)),
+            dma((3,)),
+        ],
+        compiler_params=pltpu.CompilerParams(
+            collective_id=0, has_side_effects=True, vmem_limit_bytes=48 * 1024 * 1024
+        ),
+    )(query_rows, key_rows, value_rows, id_block)
+
+
 def body(query_rows, key_rows, value_rows, span_ids):
     tokens = query_rows.shape[0]
+    if fits_kernel(query_rows, key_rows):
+        return fused(query_rows, key_rows, value_rows, span_ids)
     span_len = tokens // 2
     kv_heads = key_rows.shape[1] // HEAD_DIM
     key_count = key_rows.shape[0]

time: 139 us -> 47.2 us (0.34)
  Pallas kernels: 0 us -> 42.3 us
  waiting for transfers between devices: 36.3 us -> 0 us
  other arithmetic: 24.9 us -> 0 us
  matrix products: 20.7 us -> 0 us
  local copies, waits for them, and re-layouts: 21.5 us -> 4.61 us
  between operations: 14.1 us -> 0.01 us
  blocking collectives: 12.8 us -> 0 us
  starting transfers between devices: 7.64 us -> 0 us
    pallas_call x0 -> x1, Pallas kernels: none -> 42.3 us  [fused(): pl.pallas_call(functools.partial(attention_kernel, planes, span, per_kv,...]
    all_gather x1 -> x0, waiting for transfers between devices: 29.2 us -> none  [body(): lax.all_gather(paired, 'blk', axis=1, tiled=True)]
    dot_general x12 -> x0, matrix products: 20.7 us -> none  [the longest x6 13.9 us: attend(): jnp.einsum('grtn,ngd->grtd', weights, values_block, preferred_element_typ...]
    unnamed x1 -> x0, blocking collectives: 12.8 us -> none
    reduce_sum x12 -> x0, other arithmetic: 12.6 us -> none  [the longest x6 12 us: attend(): total = total * factor + jnp.sum(weights.astype(jnp.float32), axis=-1)]
    dynamic_slice x12 -> x0, local copies, waits for them, and re-layouts: 10 us -> none  [fold_keys(): return lax.scan(step, state_in, (pieces, offsets))[0]]
    all_to_all x2 -> x0, starting transfers between devices: 7.6 us -> none  [the longest x1 4.26 us: body(): lax.all_to_all(jnp.stack(key_parts), 'grp', split_axis=0, concat_axis=1,...]
    all_to_all x2 -> x0, waiting for transfers between devices: 7.06 us -> none  [the longest x1 4.2 us: body(): lax.all_to_all(jnp.stack(value_parts), 'grp', split_axis=0, concat_axis=1...]
  transfers between devices with their start and end apart: 3 -> 0, of which waited for: 3 -> 0; matrix products, arithmetic and copies ran while one was open for 4% -> 0% of each run, Pallas kernels for 0% -> 0%
where the time goes in v1:
time: 47.2 us; the launch traced here: 47 us
  Pallas kernels  42.3 us (90%)
  local copies, waits for them, and re-layouts  4.61 us (10%)
    pallas_call x1, Pallas kernels, fused(): pl.pallas_call(functools.partial(attention_kernel, planes, span, per_kv,...  42.3 us
    unnamed x7, local copies, waits for them, and re-layouts  3.8 us

profile of v1, /device:TPU:0, one launch (start us, length us, event | category | flops | bytes accessed | tf_op | source)
XLA Modules:
  0.0 47.0 jit_solution(18221237653434383191)
XLA Ops:
  0.0 0.7 %tile.2 = s32[4,2]{1,0:T(4,128)S(1)} broadcast(s32[2]{0:T(128)} %param.7), dimensions={1} | broadcast | bytes 40 | tf_op jit(solution)/shard_map/tile | solution.py:375
  0.7 0.1 broadcast_in_dim.7
  0.7 0.1 broadcast_in_dim.8.id_ref
  0.8 0.0 copy-start
  0.8 1.1 %copy-done = bf16[192,2048]{1,0:T(8,128)(2,1)S(1)} copy-done((bf16[192,2048]{1,0:T(8,128)(2,1)S(1)}, bf16[192,2048]{1,0:T(8,128)(2,1)}, u32[]{:S(2)}) %copy-start) | copy-done | bytes 786456
  2.0 0.0 copy-start.1
  2.0 0.9 %copy-done.1 = bf16[96,512]{1,0:T(8,128)(2,1)S(1)} copy-done((bf16[96,512]{1,0:T(8,128)(2,1)S(1)}, bf16[96,512]{1,0:T(8,128)(2,1)}, u32[]{:S(2)}) %copy-start.1) | copy-done | bytes 98328
  2.8 0.0 copy-start.2
  2.8 0.9 %copy-done.2 = bf16[96,512]{1,0:T(8,128)(2,1)S(1)} copy-done((bf16[96,512]{1,0:T(8,128)(2,1)S(1)}, bf16[96,512]{1,0:T(8,128)(2,1)}, u32[]{:S(2)}) %copy-start.2) | copy-done | bytes 98328
  3.7 42.3 %shard_map.46 = bf16[192,2048]{1,0:T(8,128)(2,1)S(1)} custom-call(bf16[192,2048]{1,0:T(8,128)(2,1)S(1)} %copy-done, bf16[96,512]{1,0:T(8,128)(2,1)S(1)} %copy-done.1, bf16[96,512]{1,0:T(8,128)(2,1)S(1)} %copy-done.2, s32[8,128]{1,0:T(8,128)S(1)} %broadcast_in_dim.8.id_ref), custom_call_target="tpu_custom_call" | custom-call | tf_op jit(solution)/shard_map/pallas_call | solution.py:379
  46.1 0.9 %copy.6 = bf16[192,2048]{1,0:T(8,128)(2,1)} copy(bf16[192,2048]{1,0:T(8,128)(2,1)S(1)} %shard_map.46) | data formatting | bytes 1572864
Async XLA Ops:
  0.8 1.1 %copy-start = (bf16[192,2048]{1,0:T(8,128)(2,1)S(1)}, bf16[192,2048]{1,0:T(8,128)(2,1)}, u32[]{:S(2)}) copy-start(bf16[192,2048]{1,0:T(8,128)(2,1)} %q_hbm.1) | copy-start | bytes 2359300
  2.0 0.9 %copy-start.1 = (bf16[96,512]{1,0:T(8,128)(2,1)S(1)}, bf16[96,512]{1,0:T(8,128)(2,1)}, u32[]{:S(2)}) copy-start(bf16[96,512]{1,0:T(8,128)(2,1)} %k_hbm.1) | copy-start | bytes 294916
  2.8 0.9 %copy-start.2 = (bf16[96,512]{1,0:T(8,128)(2,1)S(1)}, bf16[96,512]{1,0:T(8,128)(2,1)}, u32[]{:S(2)}) copy-start(bf16[96,512]{1,0:T(8,128)(2,1)} %v_hbm.1) | copy-start | bytes 294916

commit v2 on v1

--- a/solution.py
+++ b/solution.py
@@ -93,8 +93,8 @@
 
 def attention_kernel(
     planes, span, per_kv, rows_at_once,
-    q_hbm, k_hbm, v_hbm, id_ref, out_ref,
-    kv, stage, ids, qraw, qaug_q, kp, vp, onehot, acc, mark, obuf,
+    q_hbm, k_hbm, v_hbm, id_in, out_ref,
+    id_ref, kv, stage, ids, qraw, qaug_q, kp, vp, onehot, acc, mark, obuf,
     load_sem, swap_send, swap_recv, id_send, id_recv, q_sem,
     up_send, down_send, x_send, z_recv, x_recv, out_sem,
 ):
@@ -140,6 +140,9 @@
     for half in range(2):
         load_own(half).start()
 
+    for s in range(2):
+        id_ref[s : s + 1, :] = jnp.full((1, HEAD_DIM), id_in[s], jnp.int32)
+
     barrier = pltpu.get_barrier_semaphore()
 
     @pl.loop(1, blocks)
@@ -159,8 +162,8 @@
     penalty = jnp.where(
         ((lane > token) & (lane < span)) | (lane == span), FAR, 0.0
     ).astype(jnp.bfloat16)
-    for slot in range(4):
-        for r in range(per_kv):
+    for slot in range(2):
+        for r in range(2 * per_kv):
             qaug_q[slot, r * span : (r + 1) * span, HEAD_DIM:] = penalty
     vp[:, HEAD_DIM:] = jnp.ones((keys, HEAD_DIM), jnp.bfloat16)
     mark[...] = jnp.full(mark.shape, -3e38, jnp.float32)
@@ -257,7 +260,8 @@
     for slot in range(4):
         s = slot % 2
         for r in range(per_kv):
-            qaug_q[slot, r * span : (r + 1) * span, :HEAD_DIM] = qraw[
+            at = (s * per_kv + r) * span
+            qaug_q[slot // 2, at : at + span, :HEAD_DIM] = qraw[
                 slot // 2, s * span : (s + 1) * span, r * HEAD_DIM : (r + 1) * HEAD_DIM
             ]
     own_id.wait()
@@ -276,67 +280,76 @@
         inner = z + jnp.where(k % 2 == 1, -half, half)
         return jnp.where(k <= 2 * near, inner, z + sign * (k - near))
 
-    def finish(slot):
-        s = slot % 2
-        for r in range(per_kv):
-            both = acc[slot, r * span : (r + 1) * span, :]
-            obuf[slot // 2, pl.ds(pl.multiple_of(s * span, 16), span), r * HEAD_DIM : (r + 1) * HEAD_DIM] = (
-                both[:, :HEAD_DIM] / both[:, HEAD_DIM:]
-            ).astype(jnp.bfloat16)
+    def finish(half):
+        for s in range(2):
+            for r in range(per_kv):
+                both = acc[half, (s * per_kv + r) * span : (s * per_kv + r + 1) * span, :]
+                obuf[half, s * span : (s + 1) * span, r * HEAD_DIM : (r + 1) * HEAD_DIM] = (
+                    both[:, :HEAD_DIM] / both[:, HEAD_DIM:]
+                ).astype(jnp.bfloat16)
 
     out_away = remote(obuf.at[0], out_ref.at[:, q_columns(c)], out_sem.at[0], out_sem.at[1], sibling)
     out_here = pltpu.make_async_copy(obuf.at[1], out_ref.at[:, q_columns(c)], out_sem.at[2])
 
-    @pl.loop(0, 4 * planes)
+    @pl.loop(0, 2 * planes)
     def _(t):
-        k, slot = t // 4, t % 4
+        k, half = t // 2, t % 2
         p = plane_of(k)
 
-        @pl.when(slot == 0)
+        @pl.when(half == 0)
         def _():
             service(k + 1, y)
             x_arrival(p, y).wait_recv()
             x_arrival(p, other_y).wait_recv()
             plane = kv[p].reshape(keys, 2 * HEAD_DIM)
-            kp[:, :HEAD_DIM] = plane[:, :HEAD_DIM]
+            kp[0, :, :HEAD_DIM] = plane[:, :HEAD_DIM]
+            kp[1, :, :HEAD_DIM] = plane[:, :HEAD_DIM]
             vp[:, :HEAD_DIM] = plane[:, HEAD_DIM:]
 
-        @pl.when(slot == 2)
+        @pl.when(half == 1)
         def _():
             service(k + 1, other_y)
 
-        owner = z * 4 + x * 2 + jnp.where(slot < 2, other_c, c)
-        id_q = ids[owner, pl.ds(slot % 2, 1), :]
-        for j in range(8):
-            kx, ky, kc = j // 4, (j // 2) % 2, j % 2
-            id_k = ids[ky * (blocks // 2) + p * 2 + kx, kc : kc + 1, :]
-            same = jnp.where(id_k == id_q, 1.0, 0.0)
-            later = jnp.where(id_k > id_q, 1.0, 0.0)
-            choice = jnp.where(lane_row < span, same, later).astype(jnp.bfloat16)
-            kp[j * span : (j + 1) * span, HEAD_DIM:] = onehot[...] * choice
-
-        kmat = kp[...]
+        owner = z * 4 + x * 2 + jnp.where(half == 0, other_c, c)
+        for s in range(2):
+            id_q = ids[owner, s : s + 1, :]
+            for j in range(8):
+                kx, ky, kc = j // 4, (j // 2) % 2, j % 2
+                id_k = ids[ky * (blocks // 2) + p * 2 + kx, kc : kc + 1, :]
+                same = jnp.where(id_k == id_q, 1.0, 0.0)
+                later = jnp.where(id_k > id_q, 1.0, 0.0)
+                choice = jnp.where(lane_row < span, same, later).astype(jnp.bfloat16)
+                kp[s, j * span : (j + 1) * span, HEAD_DIM:] = onehot[...] * choice
+
+        kmats = (kp[0], kp[1])
         vmat = vp[...]
-        for first in range(0, rows, rows_at_once):
+
+        def score(first):
+            return lax.dot_general(
+                qaug_q[half, pl.ds(first, rows_at_once), :], kmats[first // rows],
+                (((1,), (1,)), ((), ())), preferred_element_type=jnp.float32,
+            )
+
+        ahead = score(0)
+        for first in range(0, 2 * rows, rows_at_once):
             part = pl.ds(first, rows_at_once)
-            scores = lax.dot_general(
-                qaug_q[slot, part, :], kmat, (((1,), (1,)), ((), ())),
-                preferred_element_type=jnp.float32,
-            )
-            before = mark[slot, part, :]
+            scores = ahead
+            if first + rows_at_once < 2 * rows:
+                ahead = score(first + rows_at_once)
+            before = mark[half, part, :]
             fresh = jnp.maximum(before, jnp.max(scores, axis=1, keepdims=True))
-            mark[slot, part, :] = fresh
+            mark[half, part, :] = fresh
             weights = jnp.exp2((scores - fresh[:, :1]) * factor).astype(jnp.bfloat16)
             fade = jnp.exp2((before - fresh) * factor)
             update = jnp.dot(weights, vmat, preferred_element_type=jnp.float32)
-            acc[slot, part, :HEAD_DIM] = acc[slot, part, :HEAD_DIM] * fade + update[:, :HEAD_DIM]
-            acc[slot, part, HEAD_DIM:] = acc[slot, part, HEAD_DIM:] * fade + update[:, HEAD_DIM:]
+            acc[half, part, :HEAD_DIM] = acc[half, part, :HEAD_DIM] * fade + update[:, :HEAD_DIM]
+            acc[half, part, HEAD_DIM:] = acc[half, part, HEAD_DIM:] * fade + update[:, HEAD_DIM:]
 
         @pl.when(k == planes - 1)
         def _():
-            finish(slot)
-
-        @pl.when((k == planes - 1) & (slot == 2))
+            finish(half)
+
+        @pl.when((k == planes - 1) & (half == 0))
         def _():
             out_away.start()
 
@@ -372,26 +385,26 @@
     span = tokens // 2
     per_kv = columns // (2 * HEAD_DIM)
     rows, keys, wide = per_kv * span, 8 * span, per_kv * HEAD_DIM
-    id_block = jnp.broadcast_to(jnp.tile(span_ids, 4)[:, None], (8, HEAD_DIM))
     dma = pltpu.SemaphoreType.DMA
-    anywhere = pl.BlockSpec(memory_space=pl.ANY)
+    hbm = pl.BlockSpec(memory_space=pltpu.HBM)
     bf16, f32 = jnp.bfloat16, jnp.float32
     return pl.pallas_call(
         functools.partial(attention_kernel, planes, span, per_kv, math.gcd(rows, 256)),
         out_shape=jax.ShapeDtypeStruct((tokens, columns), bf16),
-        in_specs=[anywhere] * 3 + [pl.BlockSpec(memory_space=pltpu.VMEM)],
-        out_specs=anywhere,
+        in_specs=[hbm] * 3 + [pl.BlockSpec(memory_space=pltpu.SMEM)],
+        out_specs=pl.BlockSpec(memory_space=pl.ANY),
         scratch_shapes=[
+            pltpu.VMEM((8, HEAD_DIM), jnp.int32),
             pltpu.VMEM((planes, 2, 2, 2, span, 2 * HEAD_DIM), bf16),
             pltpu.VMEM((4, span, 2 * HEAD_DIM), bf16),
             pltpu.VMEM((4 * planes, 8, HEAD_DIM), jnp.int32),
             pltpu.VMEM((2, tokens, wide), bf16),
-            pltpu.VMEM((4, rows, 2 * HEAD_DIM), bf16),
-            pltpu.VMEM((keys, 2 * HEAD_DIM), bf16),
+            pltpu.VMEM((2, 2 * rows, 2 * HEAD_DIM), bf16),
+            pltpu.VMEM((2, keys, 2 * HEAD_DIM), bf16),
             pltpu.VMEM((keys, 2 * HEAD_DIM), bf16),
             pltpu.VMEM((span, HEAD_DIM), bf16),
-            pltpu.VMEM((4, rows, 2 * HEAD_DIM), f32),
-            pltpu.VMEM((4, rows, HEAD_DIM), f32),
+            pltpu.VMEM((2, 2 * rows, 2 * HEAD_DIM), f32),
+            pltpu.VMEM((2, 2 * rows, HEAD_DIM), f32),
             pltpu.VMEM((2, tokens, wide), bf16),
             dma((5, 2)),
             dma((3,)),
@@ -407,9 +420,9 @@
             dma((3,)),
         ],
         compiler_params=pltpu.CompilerParams(
-            collective_id=0, has_side_effects=True, vmem_limit_bytes=48 * 1024 * 1024
+            collective_id=0, has_side_effects=True, vmem_limit_bytes=67_000_000
         ),
-    )(query_rows, key_rows, value_rows, id_block)
+    )(query_rows, key_rows, value_rows, span_ids)
 
 
 def body(query_rows, key_rows, value_rows, span_ids):

time: 47.2 us -> 42.4 us (0.90)
  local copies, waits for them, and re-layouts: 4.61 us -> 2.09 us
  Pallas kernels: 42.3 us -> 40 us
    pallas_call x1, Pallas kernels: 42.3 us -> 40 us  [fused(): pl.pallas_call(functools.partial(attention_kernel, planes, span, per_kv,...]
    unnamed x7 -> x1, local copies, waits for them, and re-layouts: 3.8 us -> 2.09 us
    another operation x1 -> x0, local copies, waits for them, and re-layouts: 0.66 us -> none  [fused(): id_block = jnp.broadcast_to(jnp.tile(span_ids, 4)[:, None], (8, HEAD_DIM))]
where the time goes in v2:
time: 42.4 us; the launch traced here: 42.1 us
  Pallas kernels  40 us (94%)
  local copies, waits for them, and re-layouts  2.09 us (5%)
    pallas_call x1, Pallas kernels, fused(): pl.pallas_call(functools.partial(attention_kernel, planes, span, per_kv,...  40 us
    unnamed x1, local copies, waits for them, and re-layouts  2.09 us

profile of v2, /device:TPU:0, one launch (start us, length us, event | category | flops | bytes accessed | tf_op | source)
XLA Modules:
  0.0 42.1 jit_solution(5199590082760214674)
XLA Ops:
  0.0 40.0 %shard_map.46 = bf16[192,2048]{1,0:T(8,128)(2,1)} custom-call(bf16[192,2048]{1,0:T(8,128)(2,1)} %q_hbm.1, bf16[96,512]{1,0:T(8,128)(2,1)} %k_hbm.1, bf16[96,512]{1,0:T(8,128)(2,1)} %v_hbm.1, s32[2]{0:T(128)} %id_in.1), custom_call_target="tpu_custom_call" | custom-call | tf_op jit(solution)/shard_map/pallas_call | solution.py:391
  40.0 2.1 %copy.6 = bf16[192,2048]{1,0:T(8,128)(2,1)} copy(bf16[192,2048]{1,0:T(8,128)(2,1)} %shard_map.46) | data formatting | bytes 1572864
